TPU v7x, 32 devices: a whole 2x2x4 slice. The times are simulated.
32 devices in a mesh: seq: 4 (over y, x), batch: 8 (over z, core).
Axes of the slice: x: 2, y: 2, z: 4, core: 2. Of those that a mesh axis runs over, the one named last changes fastest.
Arguments:
- activations: bfloat16 [8, 3072, 4096], P('batch', 'seq'), may hold values from -18 to 18
- out_grads: bfloat16 [8, 3072, 4096], P('batch', 'seq'), may hold values from -0.29882812 to 0.29882812
- lengths: int32 [8, 3], P('batch'), may hold values from 1 to 1536, 3072 in all within a row
Outputs:
- act_factor: float32 [4096, 4096], P(('seq', 'batch'))
- grad_factor: float32 [4096, 4096], P(('seq', 'batch'))
Inputs may be any that keep to these rules, and one draw needn't show every extreme that they name: `lengths`: each row sums to 3072 and its largest entry is exactly 1536.
All inputs are finite; a program needn't handle non-finite values.
Results may differ from a plain program's by a relative error of at most 0.004.
Values may be sent and summed in bfloat16 or wider, within the bound.
A program may use at most 64 MiB of HBM per device.

v0:
```python
import jax
import jax.numpy as jnp
from jax import lax
from jax.sharding import PartitionSpec as P


def local(activations, out_grads, lengths):
    act_local = activations[0]
    grad_local = out_grads[0]
    seq_lengths = lengths[0]
    tok_count = act_local.shape[0]
    width = act_local.shape[1]
    seq_count = seq_lengths.shape[0]
    group_size = lax.axis_size("seq")
    devices = group_size * lax.axis_size("batch")
    tile_rows = width // devices
    tile_start = lax.axis_index(("seq", "batch")) * tile_rows
    total_seqs = seq_count * lax.axis_size("batch")
    ends = jnp.cumsum(seq_lengths)
    starts = ends - seq_lengths
    position = lax.axis_index("seq") * tok_count + jnp.arange(tok_count, dtype=jnp.int32)
    member = (position[None, :] >= starts[:, None]) & (position[None, :] < ends[:, None])
    member = member.astype(jnp.bfloat16)
    act_part = jnp.dot(member, act_local, preferred_element_type=jnp.float32)
    grad_part = jnp.dot(member, grad_local, preferred_element_type=jnp.float32)
    act_sum, grad_sum = lax.psum((act_part, grad_part), "seq")
    act_rows = (act_sum / seq_lengths[:, None].astype(jnp.float32)).astype(jnp.bfloat16)
    grad_rows = grad_sum.astype(jnp.bfloat16)
    act_piece = lax.all_gather(act_rows, "batch", axis=0, tiled=True)
    grad_piece = lax.all_gather(grad_rows, "batch", axis=0, tiled=True)
    act_cols = lax.dynamic_slice_in_dim(act_piece, tile_start, tile_rows, 1)
    grad_cols = lax.dynamic_slice_in_dim(grad_piece, tile_start, tile_rows, 1)
    dims = (((0,), (0,)), ((), ()))
    act_new = lax.dot_general(act_cols, act_piece, dims, preferred_element_type=jnp.float32)
    grad_new = lax.dot_general(grad_cols, grad_piece, dims, preferred_element_type=jnp.float32)
    return (act_new / total_seqs, grad_new / total_seqs)


def solution(mesh):
    in_specs = (P("batch", "seq", None), P("batch", "seq", None), P("batch", None))
    out_specs = (P(("seq", "batch"), None), P(("seq", "batch"), None))
    return jax.shard_map(local, mesh=mesh, in_specs=in_specs, out_specs=out_specs, check_vma=False)
```

profile of v0, /device:TPU:0, one launch (start us, length us, event | category | flops | bytes accessed | tf_op | source)
XLA Modules:
  0.0 60.4 jit_solution(18398643600127713620)
XLA Ops:
  0.6 0.8 %reduce-window.7 = s32[3,1]{0,1:T(1,128)S(1)} reduce-window(s32[3,1]{0,1:T(1,128)} %bitcast.22, s32[]{:T(128)} %constant.7.clone.1), window={size=3x1 pad=2_0x0_0}, to_apply=%region_0.0 | reduce-window | flops 6 | bytes 28 | tf_op jit(solution)/shard_map/reduce-window.2
  1.5 0.0 copy-start
  1.5 0.8 %bitcast_subtract_fusion = s32[3]{0:T(128)S(1)} fusion(s32[1,3]{1,0:T(1,128)} %param.5, s32[3,1]{0,1:T(1,128)S(1)} %reduce-window.7), kind=kLoop, calls=%fused_computation.14 | loop fusion | flops 3 | bytes 36 | tf_op jit(solution)/shard_map/sub | solution.py:20
  2.3 0.8 %bitcast_convert_fusion = f32[3]{0:T(128)S(1)} fusion(s32[1,3]{1,0:T(1,128)} %param.5), kind=kLoop, calls=%fused_computation.13 | loop fusion | flops 3 | bytes 24 | tf_op jit(solution)/shard_map/convert_element_type | solution.py:27
  3.1 4.0 %fusion = f32[3,4096]{1,0:T(4,128)S(1)} fusion(bf16[1,768,4096]{2,1,0:T(8,128)(2,1)} %param.4, s32[768]{0:T(1024)S(1)} %iota_add_fusion, s32[3]{0:T(128)S(1)} %bitcast.20, s32[3]{0:T(128)S(1)} %bitcast_subtract_fusion), kind=kOutput, calls=%fused_computation | convolution fusion | flops 18881280 | bytes 6343704 | tf_op jit(solution)/shard_map/dot_general | solution.py:25
  7.1 0.0 copy-done
  7.1 1.0 %fusion.2 = f32[3,4096]{1,0:T(4,128)S(1)} fusion(bf16[1,768,4096]{2,1,0:T(8,128)(2,1)S(1)} %copy-done, s32[768]{0:T(1024)S(1)} %iota_add_fusion, s32[3]{0:T(128)S(1)} %bitcast.21, s32[3]{0:T(128)S(1)} %bitcast_subtract_fusion), kind=kOutput, calls=%fused_computation.2 | convolution fusion | flops 18881280 | bytes 6343704 | tf_op jit(solution)/shard_map/dot_general | solution.py:24
  8.0 19.8 %all-reduce.2 = (f32[3,4096]{1,0:T(4,128)S(1)}, bf16[3,4096]{1,0:T(4,128)(2,1)S(1)}) all-reduce(f32[3,4096]{1,0:T(4,128)S(1)} %fusion.2, f32[3,4096]{1,0:T(4,128)S(1)} %fusion), channel_id=1, replica_groups=mesh['seq'=4,'batch'=8] {'seq'}, use_global_device_ids=true, to_apply=%region_1.2 | all-reduce | flops 24576 | bytes 172032 | tf_op jit(solution)/shard_map/psum | solution.py:26
  27.8 0.1 fusion.4
  27.9 14.4 %all-gather.1 = bf16[8,3,4096]{2,1,0:T(4,128)(2,1)S(1)} all-gather(bf16[1,3,4096]{2,1,0:T(4,128)(2,1)S(1)} %bitcast.19), channel_id=1, replica_groups=mesh['seq'=4,'batch'=8] {'batch'}, dimensions={0}, use_global_device_ids=true | all-gather | bytes 221184 | tf_op jit(solution)/shard_map/all_gather | solution.py:30
  42.3 0.2 reshape.48
  42.5 14.2 %all-gather = bf16[8,3,4096]{2,1,0:T(4,128)(2,1)S(1)} all-gather(bf16[1,3,4096]{2,1,0:T(4,128)(2,1)S(1)} %fusion.4), channel_id=1, replica_groups=mesh['seq'=4,'batch'=8] {'batch'}, dimensions={0}, use_global_device_ids=true | all-gather | bytes 221184 | tf_op jit(solution)/shard_map/all_gather | solution.py:29
  56.7 0.2 reshape.46
  56.9 1.8 %convolution_multiply_fusion.1 = f32[128,4096]{1,0:T(8,128)} fusion(bf16[24,4096]{1,0:T(8,128)(2,1)S(1)} %reshape.46, s32[]{:T(128)S(6)} %select_n.4), kind=kOutput, calls=%fused_computation.5 | convolution fusion | flops 25690112 | bytes 2299908 | tf_op jit(solution)/shard_map/dot_general | solution.py:34
  58.7 1.8 %convolution_multiply_fusion = f32[128,4096]{1,0:T(8,128)} fusion(bf16[24,4096]{1,0:T(8,128)(2,1)S(1)} %reshape.48, s32[]{:T(128)S(6)} %select_n.4), kind=kOutput, calls=%fused_computation.4 | convolution fusion | flops 25690112 | bytes 2299908 | tf_op jit(solution)/shard_map/dot_general | solution.py:35
  (1 shorter events, 0.0 us)
Async XLA Ops:
  1.5 5.6 %copy-start = (bf16[1,768,4096]{2,1,0:T(8,128)(2,1)S(1)}, bf16[1,768,4096]{2,1,0:T(8,128)(2,1)}, u32[]{:S(2)}) copy-start(bf16[1,768,4096]{2,1,0:T(8,128)(2,1)} %param.3) | copy-start | bytes 18874372
where the time goes:
time: 60.7 us; the launch traced here: 60.4 us
  blocking collectives  48.4 us (80%)
  matrix products  8.53 us (14%)
  other arithmetic  2.51 us (4%)
  between operations  0.67 us (1%)
    psum x1, blocking collectives, local(): act_sum, grad_sum = lax.psum((act_part, grad_part), 'seq')  19.8 us
    all_gather x1, blocking collectives, local(): grad_piece = lax.all_gather(grad_rows, 'batch', axis=0, tiled=True)  14.4 us
    all_gather x1, blocking collectives, local(): act_piece = lax.all_gather(act_rows, 'batch', axis=0, tiled=True)  14.2 us
    dot_general x1, matrix products, local(): grad_part = jnp.dot(member, grad_local, preferred_element_type=jnp.float32)  3.99 us
    dot_general x1, matrix products, local(): lax.dot_general(act_cols, act_piece, dims, preferred_element_type=jnp.flo...  1.79 us
    dot_general x1, matrix products, local(): lax.dot_general(grad_cols, grad_piece, dims, preferred_element_type=jnp.f...  1.78 us

commit v1 on v0

--- a/solution.py
+++ b/solution.py
@@ -26,8 +26,11 @@
     act_sum, grad_sum = lax.psum((act_part, grad_part), "seq")
     act_rows = (act_sum / seq_lengths[:, None].astype(jnp.float32)).astype(jnp.bfloat16)
     grad_rows = grad_sum.astype(jnp.bfloat16)
-    act_piece = lax.all_gather(act_rows, "batch", axis=0, tiled=True)
-    grad_piece = lax.all_gather(grad_rows, "batch", axis=0, tiled=True)
+    act_piece, grad_piece = jnp.split(
+        lax.all_gather(jnp.concatenate([act_rows, grad_rows], axis=1), "batch", axis=0, tiled=True),
+        [act_rows.shape[1]],
+        axis=1,
+    )
     act_cols = lax.dynamic_slice_in_dim(act_piece, tile_start, tile_rows, 1)
     grad_cols = lax.dynamic_slice_in_dim(grad_piece, tile_start, tile_rows, 1)
     dims = (((0,), (0,)), ((), ()))

time: 60.7 us -> 47.3 us (0.78)
  blocking collectives: 48.4 us -> 35 us
    all_gather x2 -> x1, blocking collectives: 28.6 us -> 15.2 us  [local(): lax.all_gather(jnp.concatenate([act_rows, grad_rows], axis=1), 'batch', a...]
where the time goes in v1:
time: 47.3 us; the launch traced here: 47.1 us
  blocking collectives  35 us (74%)
  matrix products  8.53 us (18%)
  other arithmetic  2.54 us (5%)
  between operations  0.68 us (1%)
    psum x1, blocking collectives, local(): act_sum, grad_sum = lax.psum((act_part, grad_part), 'seq')  19.7 us
    all_gather x1, blocking collectives, local(): lax.all_gather(jnp.concatenate([act_rows, grad_rows], axis=1), 'batch', a...  15.2 us
    dot_general x1, matrix products, local(): grad_part = jnp.dot(member, grad_local, preferred_element_type=jnp.float32)  3.99 us
    dot_general x1, matrix products, local(): lax.dot_general(grad_cols, grad_piece, dims, preferred_element_type=jnp.f...  1.79 us
    dot_general x1, matrix products, local(): lax.dot_general(act_cols, act_piece, dims, preferred_element_type=jnp.flo...  1.78 us
    dot_general x1, matrix products, local(): act_part = jnp.dot(member, act_local, preferred_element_type=jnp.float32)  0.96 us

profile of v1, /device:TPU:0, one launch (start us, length us, event | category | flops | bytes accessed | tf_op | source)
XLA Modules:
  0.0 47.1 jit_solution(4271760519261514999)
XLA Ops:
  0.6 0.8 %reduce-window.7 = s32[3,1]{0,1:T(1,128)S(1)} reduce-window(s32[3,1]{0,1:T(1,128)} %bitcast.18, s32[]{:T(128)} %constant.7.clone.1), window={size=3x1 pad=2_0x0_0}, to_apply=%region_0.0 | reduce-window | flops 6 | bytes 28 | tf_op jit(solution)/shard_map/reduce-window.2
  1.5 0.0 copy-start
  1.5 0.8 %bitcast_subtract_fusion = s32[3]{0:T(128)S(1)} fusion(s32[1,3]{1,0:T(1,128)} %param.5, s32[3,1]{0,1:T(1,128)S(1)} %reduce-window.7), kind=kLoop, calls=%fused_computation.13 | loop fusion | flops 3 | bytes 36 | tf_op jit(solution)/shard_map/sub | solution.py:20
  2.3 0.8 %bitcast_convert_fusion = f32[3]{0:T(128)S(1)} fusion(s32[1,3]{1,0:T(1,128)} %param.5), kind=kLoop, calls=%fused_computation.12 | loop fusion | flops 3 | bytes 24 | tf_op jit(solution)/shard_map/convert_element_type | solution.py:27
  3.1 4.0 %fusion = f32[3,4096]{1,0:T(4,128)S(1)} fusion(bf16[1,768,4096]{2,1,0:T(8,128)(2,1)} %param.4, s32[768]{0:T(1024)S(1)} %iota_add_fusion, s32[3]{0:T(128)S(1)} %bitcast.16, s32[3]{0:T(128)S(1)} %bitcast_subtract_fusion), kind=kOutput, calls=%fused_computation | convolution fusion | flops 18881280 | bytes 6343704 | tf_op jit(solution)/shard_map/dot_general | solution.py:25
  7.1 0.0 copy-done
  7.1 1.0 %fusion.2 = f32[3,4096]{1,0:T(4,128)S(1)} fusion(bf16[1,768,4096]{2,1,0:T(8,128)(2,1)S(1)} %copy-done, s32[768]{0:T(1024)S(1)} %iota_add_fusion, s32[3]{0:T(128)S(1)} %bitcast.17, s32[3]{0:T(128)S(1)} %bitcast_subtract_fusion), kind=kOutput, calls=%fused_computation.2 | convolution fusion | flops 18881280 | bytes 6343704 | tf_op jit(solution)/shard_map/dot_general | solution.py:24
  8.0 19.7 %all-reduce.2 = (bf16[3,4096]{1,0:T(4,128)(2,1)S(1)}, f32[3,4096]{1,0:T(4,128)S(1)}) all-reduce(f32[3,4096]{1,0:T(4,128)S(1)} %fusion, f32[3,4096]{1,0:T(4,128)S(1)} %fusion.2), channel_id=1, replica_groups=mesh['seq'=4,'batch'=8] {'seq'}, use_global_device_ids=true, to_apply=%region_2.3 | all-reduce | flops 24576 | bytes 172032 | tf_op jit(solution)/shard_map/psum | solution.py:26
  27.8 0.1 divide_convert_fusion
  27.9 15.2 %all-gather = bf16[8,3,8192]{2,1,0:T(4,128)(2,1)S(1)} all-gather(bf16[1,3,8192]{2,1,0:T(4,128)(2,1)S(1)} %maximum_bitcast_fusion), channel_id=1, replica_groups=mesh['seq'=4,'batch'=8] {'batch'}, dimensions={0}, use_global_device_ids=true | all-gather | bytes 442368 | tf_op jit(solution)/shard_map/all_gather | solution.py:30
  43.1 0.3 reshape.46
  43.5 1.8 %convolution_multiply_fusion = f32[128,4096]{1,0:T(8,128)} fusion(bf16[24,4096]{1,0:T(8,128)(2,1)S(1)} %get-tuple-element.4, s32[]{:T(128)S(6)} %select_n.4), kind=kOutput, calls=%fused_computation.4 | convolution fusion | flops 25690112 | bytes 2299908 | tf_op jit(solution)/shard_map/dot_general | solution.py:38
  45.3 1.8 %convolution_multiply_fusion.1 = f32[128,4096]{1,0:T(8,128)} fusion(bf16[24,4096]{1,0:T(8,128)(2,1)S(1)} %get-tuple-element.5, s32[]{:T(128)S(6)} %select_n.4), kind=kOutput, calls=%fused_computation.5 | convolution fusion | flops 25690112 | bytes 2299908 | tf_op jit(solution)/shard_map/dot_general | solution.py:37
  (3 shorter events, 0.1 us)
Async XLA Ops:
  1.5 5.6 %copy-start = (bf16[1,768,4096]{2,1,0:T(8,128)(2,1)S(1)}, bf16[1,768,4096]{2,1,0:T(8,128)(2,1)}, u32[]{:S(2)}) copy-start(bf16[1,768,4096]{2,1,0:T(8,128)(2,1)} %param.3) | copy-start | bytes 18874372
